TPU v7x, 32 devices: a whole 2x2x4 slice. The times are simulated.
32 devices in a mesh: obs: 8 (over z, y), chan: 4 (over x, core).
Axes of the slice: x: 2, y: 2, z: 4, core: 2. Of those that a mesh axis runs over, the one named last changes fastest.
Arguments:
- jacobian: bfloat16 [2048, 128, 137], P('obs', 'chan'), may hold values from -0.5 to 0.5
- departures: float32 [128, 2048], P('chan', 'obs'), may hold values from -6 to 6
- obs_weights: float32 [128, 2048], P('chan', 'obs'), may hold values from 0.25 to 4
- column_count: int32 [8], P('obs'), may hold values from 1 to 256, as said below
- grid_block: int32 [16], P('obs'), may hold values from 0 to 15, as said below
- sqrt_cov: float32 [137, 137], replicated, may hold values from -0.5 to 0.5
Outputs:
- increment: float32 [2048, 137], P('obs')
- residual: float32 [2048, 137], P('obs')
Inputs may be any that keep to these rules, and one draw needn't show every extreme that they name: The first column_count of a device's 256 column slots are observed; some device has all 256 observed in every draw. `grid_block`: the owner of grid block g is index g // 2 of obs. The 2 blocks of one device match blocks of 2 different owners; in every draw some owner has a block matched by each device (every device matches one of that owner's blocks), and some device matches that owner's last block.
All inputs are finite; a program needn't handle non-finite values.
Results may differ from a plain program's by a relative error of at most 0.02.
Values may be sent and summed in bfloat16 or wider, within the bound.
A program may use at most 64 MiB of HBM per device.

v0:
```python
import jax
import jax.numpy as jnp
from jax import lax
from jax.sharding import PartitionSpec as P

BLOCK = 128
ITERS = 5
GRID_BLK = 2


def block_terms(jac_part, weight_part, mask_part, predicted):
    scaled = (mask_part[:, None] * weight_part * predicted).astype(jnp.bfloat16)
    return lax.dot_general(
        jac_part, scaled, (((1,), (1,)), ((0,), (0,))), preferred_element_type=jnp.float32
    )


def forward_terms(jac_part, weight_part, mask_part, field_part):
    predicted = lax.dot_general(
        jac_part, field_part, (((2,), (1,)), ((0,), (0,))), preferred_element_type=jnp.float32
    )
    return block_terms(jac_part, weight_part, mask_part, predicted)


def per_device(jacobian, departures, obs_weights, column_count, grid_block, sqrt_cov):
    obs_count = lax.axis_size("obs")
    myself = lax.axis_index("obs")
    capacity, group_channels, layers = jacobian.shape
    block_count = capacity // BLOCK
    weight_cols = obs_weights.T
    depart_cols = departures.T
    observed = (jnp.arange(capacity, dtype=jnp.int32) < column_count[0]).astype(jnp.float32)
    every_id = lax.all_gather(grid_block, "obs", axis=0, tiled=True).reshape(obs_count, block_count)
    targets = jnp.arange(obs_count, dtype=jnp.int32)
    send_pick = (grid_block[None, :] // GRID_BLK == targets[:, None]).astype(jnp.float32)
    owned_here = every_id // GRID_BLK == myself
    places = every_id % GRID_BLK
    grid_index = jnp.arange(GRID_BLK, dtype=jnp.int32)
    take_pick = jnp.sum(
        ((places[None] == grid_index[:, None, None]) & owned_here[None]).astype(jnp.float32), axis=2
    )
    share_cols = BLOCK

    def local_terms(kernel_fn, inputs):
        return kernel_fn(jacobian, weight_cols, observed, inputs)

    def to_owners(terms):
        blocked = terms.reshape(block_count, BLOCK, layers)
        blocked = lax.psum(blocked, "chan")
        outgoing = jnp.dot(
            send_pick, blocked.reshape(block_count, -1), precision=lax.Precision.HIGHEST
        )
        incoming = lax.all_to_all(
            outgoing.reshape(obs_count, share_cols, layers),
            "obs",
            split_axis=0,
            concat_axis=0,
            tiled=True,
        )
        summed = jnp.dot(
            take_pick, incoming.reshape(obs_count, -1), precision=lax.Precision.HIGHEST
        )
        return summed.reshape(GRID_BLK, share_cols, layers)

    def spread(field):
        return jnp.dot(
            field.reshape(-1, layers), sqrt_cov, precision=lax.Precision.HIGHEST
        ).reshape(field.shape)

    def spread_back(field):
        flat = lax.dot_general(
            field.reshape(-1, layers),
            sqrt_cov,
            (((1,), (1,)), ((), ())),
            precision=lax.Precision.HIGHEST,
        )
        return flat.reshape(field.shape)

    def squared(values):
        partial_sum = jnp.sum(values * values)
        return lax.psum(partial_sum, "obs")

    residual = spread_back(to_owners(local_terms(block_terms, depart_cols)))
    control = jnp.zeros_like(residual)
    direction = residual
    norm_now = squared(residual)
    for iteration in range(ITERS):
        rounded = spread(direction).astype(jnp.bfloat16).reshape(GRID_BLK, -1)
        to_outgoing = jnp.dot(
            take_pick.T.astype(jnp.bfloat16), rounded, preferred_element_type=jnp.float32
        ).astype(jnp.bfloat16)
        to_incoming = lax.all_to_all(
            to_outgoing.reshape(obs_count, share_cols, layers),
            "obs",
            split_axis=0,
            concat_axis=0,
            tiled=True,
        )
        picked = jnp.dot(
            send_pick.T.astype(jnp.bfloat16),
            to_incoming.reshape(obs_count, -1),
            preferred_element_type=jnp.float32,
        )
        picked = picked.astype(jnp.bfloat16).reshape(block_count, share_cols, layers)
        fetched = picked.reshape(capacity, layers)
        image = direction + spread_back(to_owners(local_terms(forward_terms, fetched)))
        curvature_partial_sum = jnp.sum(direction * image)
        step_length = norm_now / lax.psum(curvature_partial_sum, "obs")
        control = control + step_length * direction
        residual = residual - step_length * image
        norm_next = squared(residual)
        direction = residual + norm_next / norm_now * direction
        norm_now = norm_next
    increment = spread(control)
    return (increment.reshape(-1, layers), residual.reshape(-1, layers))


def solution(mesh):
    in_specs = (P("obs", "chan", None), P("chan", "obs"), P("chan", "obs"), P("obs"), P("obs"), P())
    out_specs = (P("obs", None), P("obs", None))
    return jax.shard_map(
        per_device, mesh=mesh, in_specs=in_specs, out_specs=out_specs, check_vma=False
    )
```

profile of v0, /device:TPU:0, one launch (start us, length us, event | category | flops | bytes accessed | tf_op | source)
XLA Modules:
  0.0 699.7 jit_solution(8581663738396648842)
XLA Ops:
  13.1 33.3 %all-reduce.9.cloned.1.call-done = f32[128,137,2]{0,2,1:T(2,128)} async-done(((f32[128,137,2]{0,2,1:T(2,128)}), f32[128,137,2]{0,2,1:T(2,128)}) %all-reduce.9.cloned.1.call-update) | async-done | bytes 140304 | tf_op jit(solution)/shard_map/psum | solution.py:49
  55.7 14.9 %all-reduce = s32[16]{0:T(128)S(1)} all-reduce(s32[16]{0:T(128)S(1)} %dynamic-update-slice), channel_id=1, replica_groups=mesh['obs'=8,'chan'=4] {'obs'}, use_global_device_ids=true, to_apply=%add | all-reduce | flops 16 | bytes 128
  77.3 14.5 %all_to_all.55 = bf16[8,128,137]{1,2,0:T(8,128)(2,1)} all-to-all(bf16[8,128,137]{1,2,0:T(8,128)(2,1)} %copy.105), channel_id=1, replica_groups=mesh['obs'=8,'chan'=4] {'obs'}, dimensions={0} | all-to-all | bytes 561152 | tf_op jit(solution)/shard_map/all_to_all | solution.py:92
  99.4 27.9 %all-reduce.11.cloned.1.call-done = f32[128,137,2]{0,2,1:T(2,128)} async-done(((f32[128,137,2]{0,2,1:T(2,128)}), f32[128,137,2]{0,2,1:T(2,128)}) %all-reduce.11.cloned.1.call-update) | async-done | bytes 140304 | tf_op jit(solution)/shard_map/psum | solution.py:49
  135.3 16.2 %all-to-all-done.2 = f32[8,128,137]{1,2,0:T(8,128)S(1)} async-done(((f32[8,128,137]{1,2,0:T(8,128)}), f32[8,128,137]{1,2,0:T(8,128)S(1)}, u32[]{:S(2)}, u32[]{:S(2)}) %all-to-all-start.2) | async-done | bytes 561184 | tf_op jit(solution)/shard_map/all_to_all | solution.py:53
  159.8 20.1 %all-reduce.1 = (f32[]{:T(128)}, f32[]{:T(128)}) all-reduce(f32[]{:T(128)} %get-tuple-element.10, f32[]{:T(128)} %get-tuple-element.12), channel_id=1, replica_groups=mesh['obs'=8,'chan'=4] {'obs'}, use_global_device_ids=true, to_apply=%region_3.4 | all-reduce | flops 2 | bytes 16 | tf_op jit(solution)/shard_map/psum | solution.py:81
  181.9 17.7 %psum.116 = f32[]{:T(128)} all-reduce(f32[]{:T(128)} %multiply_reduce_fusion.7), channel_id=1, replica_groups=mesh['obs'=8,'chan'=4] {'obs'}, use_global_device_ids=true, to_apply=%region_8.9 | all-reduce | flops 1 | bytes 8 | tf_op jit(solution)/shard_map/psum | solution.py:81
  206.1 13.2 %all_to_all.56 = bf16[8,128,137]{1,2,0:T(8,128)(2,1)} all-to-all(bf16[8,128,137]{1,2,0:T(8,128)(2,1)} %copy.119), channel_id=1, replica_groups=mesh['obs'=8,'chan'=4] {'obs'}, dimensions={0} | all-to-all | bytes 561152 | tf_op jit(solution)/shard_map/all_to_all | solution.py:92
  227.0 27.8 %all-reduce.13.cloned.1.call-done = f32[128,137,2]{0,2,1:T(2,128)} async-done(((f32[128,137,2]{0,2,1:T(2,128)}), f32[128,137,2]{0,2,1:T(2,128)}) %all-reduce.13.cloned.1.call-update) | async-done | bytes 140304 | tf_op jit(solution)/shard_map/psum | solution.py:49
  256.4 22.2 %all_to_all.57 = f32[8,128,137]{1,2,0:T(8,128)S(1)} all-to-all(f32[8,128,137]{1,2,0:T(8,128)S(1)} %copy.122), channel_id=1, replica_groups=mesh['obs'=8,'chan'=4] {'obs'}, dimensions={0} | all-to-all | bytes 1122304 | tf_op jit(solution)/shard_map/all_to_all | solution.py:53
  286.9 19.5 %psum.118 = f32[]{:T(128)} all-reduce(f32[]{:T(128)} %get-tuple-element.14), channel_id=1, replica_groups=mesh['obs'=8,'chan'=4] {'obs'}, use_global_device_ids=true, to_apply=%region_11.12 | all-reduce | flops 1 | bytes 8 | tf_op jit(solution)/shard_map/psum | solution.py:108
  308.3 18.1 %psum.119 = f32[]{:T(128)} all-reduce(f32[]{:T(128)} %get-tuple-element.8), channel_id=1, replica_groups=mesh['obs'=8,'chan'=4] {'obs'}, use_global_device_ids=true, to_apply=%region_13.14 | all-reduce | flops 1 | bytes 8 | tf_op jit(solution)/shard_map/psum | solution.py:81
  353.5 27.8 %all-reduce.15.cloned.1.call-done = f32[128,137,2]{0,2,1:T(2,128)} async-done(((f32[128,137,2]{0,2,1:T(2,128)}), f32[128,137,2]{0,2,1:T(2,128)}) %all-reduce.15.cloned.1.call-update) | async-done | bytes 140304 | tf_op jit(solution)/shard_map/psum | solution.py:49
  382.8 22.2 %all_to_all.59 = f32[8,128,137]{1,2,0:T(8,128)S(1)} all-to-all(f32[8,128,137]{1,2,0:T(8,128)S(1)} %copy.131), channel_id=1, replica_groups=mesh['obs'=8,'chan'=4] {'obs'}, dimensions={0} | all-to-all | bytes 1122304 | tf_op jit(solution)/shard_map/all_to_all | solution.py:53
  413.4 19.5 %psum.121 = f32[]{:T(128)} all-reduce(f32[]{:T(128)} %get-tuple-element.16), channel_id=1, replica_groups=mesh['obs'=8,'chan'=4] {'obs'}, use_global_device_ids=true, to_apply=%region_16.17 | all-reduce | flops 1 | bytes 8 | tf_op jit(solution)/shard_map/psum | solution.py:108
  434.9 18.1 %psum.122 = f32[]{:T(128)} all-reduce(f32[]{:T(128)} %get-tuple-element.6), channel_id=1, replica_groups=mesh['obs'=8,'chan'=4] {'obs'}, use_global_device_ids=true, to_apply=%region_18.19 | all-reduce | flops 1 | bytes 8 | tf_op jit(solution)/shard_map/psum | solution.py:81
  480.2 27.8 %all-reduce.17.cloned.1.call-done = f32[128,137,2]{0,2,1:T(2,128)} async-done(((f32[128,137,2]{0,2,1:T(2,128)}), f32[128,137,2]{0,2,1:T(2,128)}) %all-reduce.17.cloned.1.call-update) | async-done | bytes 140304 | tf_op jit(solution)/shard_map/psum | solution.py:49
  509.6 22.3 %all_to_all.61 = f32[8,128,137]{1,2,0:T(8,128)} all-to-all(f32[8,128,137]{1,2,0:T(8,128)S(1)} %copy.140), channel_id=1, replica_groups=mesh['obs'=8,'chan'=4] {'obs'}, dimensions={0} | all-to-all | bytes 1122304 | tf_op jit(solution)/shard_map/all_to_all | solution.py:53
  541.3 19.5 %psum.124 = f32[]{:T(128)} all-reduce(f32[]{:T(128)} %get-tuple-element.18), channel_id=1, replica_groups=mesh['obs'=8,'chan'=4] {'obs'}, use_global_device_ids=true, to_apply=%region_21.22 | all-reduce | flops 1 | bytes 8 | tf_op jit(solution)/shard_map/psum | solution.py:108
  563.6 18.0 %psum.125 = f32[]{:T(128)} all-reduce(f32[]{:T(128)} %get-tuple-element.4), channel_id=1, replica_groups=mesh['obs'=8,'chan'=4] {'obs'}, use_global_device_ids=true, to_apply=%region_23.24 | all-reduce | flops 1 | bytes 8 | tf_op jit(solution)/shard_map/psum | solution.py:81
  589.8 13.1 %all_to_all.62 = bf16[8,128,137]{1,2,0:T(8,128)(2,1)} all-to-all(bf16[8,128,137]{1,2,0:T(8,128)(2,1)} %copy.146), channel_id=1, replica_groups=mesh['obs'=8,'chan'=4] {'obs'}, dimensions={0} | all-to-all | bytes 561152 | tf_op jit(solution)/shard_map/all_to_all | solution.py:92
  613.9 27.8 %all-reduce.19.cloned.1.call-done = f32[128,137,2]{0,2,1:T(2,128)} async-done(((f32[128,137,2]{0,2,1:T(2,128)}), f32[128,137,2]{0,2,1:T(2,128)}) %all-reduce.19.cloned.1.call-update) | async-done | bytes 140304 | tf_op jit(solution)/shard_map/psum | solution.py:49
  643.3 22.2 %all_to_all.63 = f32[8,128,137]{1,2,0:T(8,128)S(1)} all-to-all(f32[8,128,137]{1,2,0:T(8,128)S(1)} %copy.149), channel_id=1, replica_groups=mesh['obs'=8,'chan'=4] {'obs'}, dimensions={0} | all-to-all | bytes 1122304 | tf_op jit(solution)/shard_map/all_to_all | solution.py:53
  669.4 19.5 %psum.127 = f32[]{:T(128)} all-reduce(f32[]{:T(128)} %get-tuple-element.20), channel_id=1, replica_groups=mesh['obs'=8,'chan'=4] {'obs'}, use_global_device_ids=true, to_apply=%region_26.27 | all-reduce | flops 1 | bytes 8 | tf_op jit(solution)/shard_map/psum | solution.py:108
  (231 shorter events, 167.8 us)
Async XLA Ops:
  7.2 65.6 %copy-start = (f32[137,137]{1,0:T(8,128)S(1)}, f32[137,137]{1,0:T(8,128)}, u32[]{:S(2)}) copy-start(f32[137,137]{1,0:T(8,128)} %param.11) | copy-start | bytes 225232
  7.2 5.8 copy-start.19
  7.2 39.1 %all-reduce.9.cloned.1.call-start = ((), (), s32[]{:S(2)}) async-start(), calls=%async_computation.11 | async-start | bytes 280576 | tf_op jit(solution)/shard_map/psum | solution.py:49
  7.9 88.8 %copy-start.14 = (f32[256]{0:T(256)}, f32[256]{0:T(256)S(1)}, u32[]{:S(2)}) copy-start(f32[256]{0:T(256)S(1)} %compare_convert_fusion.1) | copy-start | bytes 3076
  11.4 42.9 %copy-start.20 = (u32[32]{0:T(128)S(1)}, u32[32]{0:T(128)}, u32[]{:S(2)}) copy-start(u32[32]{0:T(128)} %constant.47) | copy-start | bytes 388
  13.0 114.3 %copy-start.8 = (s32[2]{0:T(128)}, s32[2]{0:T(128)S(1)}, u32[]{:S(2)}) copy-start(s32[2]{0:T(128)S(1)} %and_select_fusion) | copy-start | bytes 28
  48.7 22.3 %all-to-all-start = ((f32[8,128,137]{1,2,0:T(8,128)}), f32[8,128,137]{1,2,0:T(8,128)S(1)}, u32[]{:S(2)}, u32[]{:S(2)}) async-start(f32[8,128,137]{1,2,0:T(8,128)} %copy.102), calls=%async_computation | async-start | bytes 1179648 | tf_op jit(solution)/shard_map/all_to_all | solution.py:53
  54.2 73.1 %all-reduce.11.cloned.1.call-start = ((), (), s32[]{:S(2)}) async-start(), calls=%async_computation.12 | async-start | bytes 280576 | tf_op jit(solution)/shard_map/psum | solution.py:49
  75.1 20.9 %copy-start.1 = (bf16[256,32,137]{0,1,2:T(8,128)(2,1)S(1)}, bf16[256,32,137]{0,1,2:T(8,128)(2,1)}, u32[]{:S(2)}) copy-start(bf16[256,32,137]{0,1,2:T(8,128)(2,1)} %param.6) | copy-start | bytes 6733828
  91.8 5.0 copy-start.5
  129.7 21.8 %all-to-all-start.2 = ((f32[8,128,137]{1,2,0:T(8,128)}), f32[8,128,137]{1,2,0:T(8,128)S(1)}, u32[]{:S(2)}, u32[]{:S(2)}) async-start(f32[8,128,137]{1,2,0:T(8,128)} %copy.108), calls=%async_computation.2 | async-start | bytes 1179648 | tf_op jit(solution)/shard_map/all_to_all | solution.py:53
  135.2 119.6 %all-reduce.13.cloned.1.call-start = ((), (), s32[]{:S(2)}) async-start(), calls=%async_computation.13 | async-start | bytes 280576 | tf_op jit(solution)/shard_map/psum | solution.py:49
  152.8 5.5 copy-start.12
  156.7 45.2 %copy-start.18 = (bf16[2,8]{1,0:T(2,128)(2,1)S(1)}, bf16[2,8]{1,0:T(2,128)(2,1)}, u32[]{:S(2)}) copy-start(bf16[2,8]{1,0:T(2,128)(2,1)} %copy-done.17) | copy-start | bytes 100
  201.5 20.3 %copy-start.9 = (s32[2]{0:T(128)S(1)}, s32[2]{0:T(128)}, u32[]{:S(2)}) copy-start(s32[2]{0:T(128)} %copy-done.8) | copy-start | bytes 28
  227.0 154.3 %all-reduce.15.cloned.1.call-start = ((), (), s32[]{:S(2)}) async-start(), calls=%async_computation.14 | async-start | bytes 280576 | tf_op jit(solution)/shard_map/psum | solution.py:49
  308.3 20.4 %copy-start.3 = (f32[2,128,137]{1,2,0:T(8,128)}, f32[2,128,137]{1,2,0:T(8,128)S(1)}, u32[]{:S(2)}) copy-start(f32[2,128,137]{1,2,0:T(8,128)S(1)} %get-tuple-element.9) | copy-start | bytes 420868
  353.5 154.6 %all-reduce.17.cloned.1.call-start = ((), (), s32[]{:S(2)}) async-start(), calls=%async_computation.15 | async-start | bytes 280576 | tf_op jit(solution)/shard_map/psum | solution.py:49
  408.1 26.1 %copy-start.4 = (f32[2,128,137]{1,2,0:T(8,128)S(1)}, f32[2,128,137]{1,2,0:T(8,128)}, u32[]{:S(2)}) copy-start(f32[2,128,137]{1,2,0:T(8,128)} %copy-done.3) | copy-start | bytes 420868
  434.9 20.4 %copy-start.2 = (f32[2,128,137]{1,2,0:T(8,128)}, f32[2,128,137]{1,2,0:T(8,128)S(1)}, u32[]{:S(2)}) copy-start(f32[2,128,137]{1,2,0:T(8,128)S(1)} %get-tuple-element.7) | copy-start | bytes 420868
  480.2 161.6 %all-reduce.19.cloned.1.call-start = ((), (), s32[]{:S(2)}) async-start(), calls=%async_computation.16 | async-start | bytes 280576 | tf_op jit(solution)/shard_map/psum | solution.py:49
  602.9 8.4 %copy-start.7 = (f32[32,256]{1,0:T(8,128)S(1)}, f32[32,256]{1,0:T(8,128)}, u32[]{:S(2)}) copy-start(f32[32,256]{1,0:T(8,128)} %param.8) | copy-start | bytes 98308
  602.9 8.4 %copy-start.16 = (f32[256]{0:T(256)S(1)}, f32[256]{0:T(256)}, u32[]{:S(2)}) copy-start(f32[256]{0:T(256)} %copy-done.14) | copy-start | bytes 3076
  611.2 30.5 %copy-start.10 = (s32[2]{0:T(128)S(1)}, s32[2]{0:T(128)}, u32[]{:S(2)}) copy-start(s32[2]{0:T(128)} %copy-done.8) | copy-start | bytes 28
  (5 other events, 16.6 us)
Sparse Core Ops, SparseCore 0:
  13.1 33.1 all-reduce.8
  99.5 27.7 all-reduce.10
  227.1 27.6 all-reduce.12
  353.6 27.6 all-reduce.14
  480.3 27.6 all-reduce.16
  614.0 27.6 all-reduce.18
where the time goes:
time: 708 us; the launch traced here: 700 us
  blocking collectives  341 us (48%)
  waiting for transfers between devices  189 us (27%)
  local copies, waits for them, and re-layouts  83.4 us (12%)
  matrix products  31.8 us (4%)
  between operations  28.7 us (4%)
  other arithmetic  15.2 us (2%)
  starting transfers between devices  11.3 us (2%)
    psum x6, waiting for transfers between devices, to_owners(): blocked = lax.psum(blocked, 'chan')  172 us
    psum x5, blocking collectives, squared(): return lax.psum(partial_sum, 'obs')  92.1 us
    all_to_all x4, blocking collectives, to_owners(): lax.all_to_all(outgoing.reshape(obs_count, share_cols, layers), 'obs', sp...  89 us
    psum x4, blocking collectives, per_device(): step_length = norm_now / lax.psum(curvature_partial_sum, 'obs')  77.8 us
    all_to_all x5, blocking collectives, per_device(): lax.all_to_all(to_outgoing.reshape(obs_count, share_cols, layers), 'obs',...  66.9 us
    dot_general x10, local copies, waits for them, and re-layouts, to_owners(): jnp.dot(take_pick, incoming.reshape(obs_count, -1), precision=lax.Precisi...  16.5 us
    all_to_all x2, waiting for transfers between devices, to_owners(): lax.all_to_all(outgoing.reshape(obs_count, share_cols, layers), 'obs', sp...  16.2 us
    reshape x10, local copies, waits for them, and re-layouts, per_device(): to_outgoing.reshape(obs_count, share_cols, layers)  15.7 us
  transfers between devices with their start and end apart: 8, of which 7 were waited for; matrix products, arithmetic and copies ran while one was open for 0% of the time, Pallas kernels for 0%

commit v1 on v0

--- a/solution.py
+++ b/solution.py
@@ -1,11 +1,16 @@
+import functools
 import jax
 import jax.numpy as jnp
 from jax import lax
+from jax.experimental import pallas as pl
+from jax.experimental.pallas import tpu as pltpu
 from jax.sharding import PartitionSpec as P
 
 BLOCK = 128
 ITERS = 5
 GRID_BLK = 2
+HIGHEST = lax.Precision.HIGHEST
+MESH = pl.DeviceIdType.MESH
 
 
 def block_terms(jac_part, weight_part, mask_part, predicted):
@@ -22,7 +27,7 @@
     return block_terms(jac_part, weight_part, mask_part, predicted)
 
 
-def per_device(jacobian, departures, obs_weights, column_count, grid_block, sqrt_cov):
+def exchange_per_step(jacobian, departures, obs_weights, column_count, grid_block, sqrt_cov):
     obs_count = lax.axis_size("obs")
     myself = lax.axis_index("obs")
     capacity, group_channels, layers = jacobian.shape
@@ -115,9 +120,195 @@
     return (increment.reshape(-1, layers), residual.reshape(-1, layers))
 
 
+def cg_kernel(
+    obs_count, chan_count, jac_ref, gram_ref, cov_ref, pick_ref, take_ref, increment_ref,
+    residual_ref, weight_ref, parts_ref, back_ref, sum_send, sum_recv, back_send, back_recv
+):
+    device_count = obs_count * chan_count
+    me = lax.axis_index("obs") * chan_count + lax.axis_index("chan")
+    rows, padded, lanes = jac_ref.shape
+    layers = increment_ref.shape[1]
+    share = BLOCK // device_count
+    grid_cols = take_ref.shape[1]
+    piece = GRID_BLK * share
+
+    def coords(target):
+        return (target // chan_count, target % chan_count)
+
+    barrier = pltpu.get_barrier_semaphore()
+
+    def greet(offset, carry):
+        pl.semaphore_signal(
+            barrier, inc=1, device_id=coords((me + offset) % device_count), device_id_type=MESH
+        )
+        return carry
+
+    lax.fori_loop(1, device_count, greet, 0)
+
+    def dot(a, b):
+        return jnp.dot(a, b, precision=HIGHEST, preferred_element_type=jnp.float32)
+
+    def source_step(n, acc):
+        kernel = jac_ref[n].astype(jnp.float32)
+        weight_ref[pl.ds(n, 1), :] = kernel[layers : layers + 1] + kernel[layers + 1 : layers + 2]
+        return acc + kernel * kernel[layers + 2 : layers + 3]
+
+    zero = jnp.zeros((padded, lanes), jnp.float32)
+    residual = dot(lax.fori_loop(0, rows, source_step, zero, unroll=4), take_ref[...])
+
+    control = direction = image = None
+    norm_last = step_last = None
+    for step in range(ITERS):
+        spread = dot(gram_ref[...], residual)
+        field = dot(spread, pick_ref[...])
+
+        def normal_step(n, acc):
+            kernel = jac_ref[n].astype(jnp.float32)
+            predicted = jnp.sum(kernel * field, axis=0, keepdims=True)
+            return acc + kernel * (predicted * weight_ref[pl.ds(n, 1), :])
+
+        terms = lax.fori_loop(0, rows, normal_step, zero, unroll=4)
+        applied = residual + dot(terms, take_ref[...])
+        norm_part = jnp.sum(residual * spread, axis=0, keepdims=True)
+        curve_part = jnp.sum(applied * spread, axis=0, keepdims=True)
+        sub = lax.broadcasted_iota(jnp.int32, (8, grid_cols), 0)
+        both = jnp.where(sub == 0, norm_part, jnp.where(sub == 1, curve_part, 0.0))
+        if grid_cols < 128:
+            both = jnp.concatenate([both, jnp.zeros((8, 128 - grid_cols), jnp.float32)], axis=1)
+        parts_ref[step, me] = both
+        if step == 0:
+            pl.semaphore_wait(barrier, device_count - 1)
+
+        def send_sum(offset, carry, step=step):
+            pltpu.make_async_remote_copy(
+                src_ref=parts_ref.at[step, me],
+                dst_ref=parts_ref.at[step, me],
+                send_sem=sum_send.at[step],
+                recv_sem=sum_recv.at[step],
+                device_id=coords((me + offset) % device_count),
+                device_id_type=MESH,
+            ).start()
+            return carry
+
+        lax.fori_loop(1, device_count, send_sum, 0)
+        others = parts_ref.at[step, pl.ds(0, device_count - 1)]
+        pltpu.make_async_copy(others, others, sum_recv.at[step]).wait()
+        pltpu.make_async_copy(others, others, sum_send.at[step]).wait()
+        total = jnp.sum(jnp.sum(parts_ref[step], axis=0), axis=1, keepdims=True)
+        norm_now, curve = total[0:1], total[1:2]
+        if step == 0:
+            length = norm_now / curve
+            direction, image = residual, applied
+            control = length * direction
+        else:
+            ratio = norm_now / norm_last
+            length = norm_now / (curve - ratio * norm_now / step_last)
+            direction = residual + ratio * direction
+            image = applied + ratio * image
+            control = control + length * direction
+        residual = residual - length * image
+        norm_last, step_last = norm_now, length
+
+    def turned(a, b):
+        return lax.dot_general(
+            a, b, (((0,), (0,)), ((), ())), precision=HIGHEST, preferred_element_type=jnp.float32
+        )
+
+    outs = (turned(control, gram_ref[...]), turned(residual, cov_ref[...]))
+    out_stage, landed = back_ref.at[0], back_ref.at[1]
+    for which, value in enumerate(outs):
+        for owner in range(obs_count):
+            out_stage[owner * chan_count, which, :, :] = value[owner * piece : (owner + 1) * piece, :layers]
+    landed[me] = out_stage[(me // chan_count) * chan_count]
+
+    def send_back(offset, carry):
+        target = (me + offset) % device_count
+        pltpu.make_async_remote_copy(
+            src_ref=out_stage.at[(target // chan_count) * chan_count],
+            dst_ref=landed.at[me],
+            send_sem=back_send,
+            recv_sem=back_recv,
+            device_id=coords(target),
+            device_id_type=MESH,
+        ).start()
+        return carry
+
+    lax.fori_loop(1, device_count, send_back, 0)
+    others = landed.at[pl.ds(0, device_count - 1)]
+    pltpu.make_async_copy(others, others, back_recv).wait()
+    pltpu.make_async_copy(others, others, back_send).wait()
+    for which, out_ref in enumerate((increment_ref, residual_ref)):
+        for block in range(GRID_BLK):
+            for source in range(device_count):
+                first = block * BLOCK + source * share
+                out_ref[first : first + share, :] = landed[
+                    source, which, block * share : (block + 1) * share, :
+                ]
+
+
+def shared_columns(jacobian, departures, obs_weights, column_count, grid_block, sqrt_cov):
+    obs_count, chan_count = lax.axis_size("obs"), lax.axis_size("chan")
+    device_count = obs_count * chan_count
+    capacity, group_channels, layers = jacobian.shape
+    block_count = capacity // BLOCK
+    share = BLOCK // device_count
+    padded = -(-(layers + 3) // 16) * 16
+    cols = obs_count * block_count * share
+    halves = 1
+    while halves * 2 * cols <= 128 and chan_count % (halves * 2) == 0:
+        halves *= 2
+    grid_total = GRID_BLK * obs_count
+
+    observed = (jnp.arange(capacity, dtype=jnp.int32) < column_count[0]).astype(jnp.float32)
+    weight = observed[:, None] * obs_weights.T
+    weight_high = weight.astype(jnp.bfloat16)
+    weight_low = (weight - weight_high.astype(jnp.float32)).astype(jnp.bfloat16)
+    source = (weight * departures.T).astype(jnp.bfloat16)
+    extra = jnp.stack([weight_high, weight_low, source], axis=2)
+    packed = jnp.concatenate([jacobian, extra], axis=2)
+    packed = jnp.pad(packed, ((0, 0), (0, 0), (0, padded - layers - 3)))
+    packed = packed.reshape(block_count, device_count, share * group_channels * padded)
+    packed = packed.transpose(1, 0, 2).reshape(device_count, -1, 128)
+    packed = lax.all_to_all(packed, ("obs", "chan"), split_axis=0, concat_axis=0, tiled=True)
+    packed = packed.reshape(
+        obs_count, halves, chan_count // halves, block_count * share, group_channels, padded
+    )
+    jac = packed.transpose(2, 4, 5, 1, 0, 3).reshape(-1, padded, halves * cols)
+
+    every_id = lax.all_gather(grid_block, "obs", axis=0, tiled=True)
+    hit = every_id[:, None] == jnp.arange(grid_total, dtype=jnp.int32)[None, :]
+    same = jnp.eye(share, dtype=jnp.bool_)
+    take = (hit[:, None, :, None] & same[None, :, None, :]).astype(jnp.float32)
+    take = take.reshape(cols, grid_total * share)
+    take = jnp.concatenate([take] * halves, axis=0)
+    fill = padded - layers
+    gram = jnp.dot(sqrt_cov.T, sqrt_cov, precision=HIGHEST)
+    gram = jnp.pad(gram, ((0, fill), (0, fill)))
+    cov = jnp.pad(sqrt_cov.T, ((0, fill), (0, fill)))
+
+    out = jax.ShapeDtypeStruct((GRID_BLK * BLOCK, layers), jnp.float32)
+    vmem = pl.BlockSpec(memory_space=pltpu.VMEM)
+    return pl.pallas_call(
+        functools.partial(cg_kernel, obs_count, chan_count),
+        out_shape=(out, out),
+        in_specs=[vmem] * 5,
+        out_specs=(vmem, vmem),
+        scratch_shapes=[
+            pltpu.VMEM((jac.shape[0], jac.shape[2]), jnp.float32),
+            pltpu.VMEM((ITERS, device_count, 8, 128), jnp.float32),
+            pltpu.VMEM((2, device_count, 2, GRID_BLK * share, layers), jnp.float32),
+            pltpu.SemaphoreType.DMA((ITERS,)),
+            pltpu.SemaphoreType.DMA((ITERS,)),
+            pltpu.SemaphoreType.DMA,
+            pltpu.SemaphoreType.DMA,
+        ],
+        compiler_params=pltpu.CompilerParams(collective_id=0, has_side_effects=True),
+    )(jac, gram, cov, take.T, take)
+
+
 def solution(mesh):
+    device_count = mesh.shape["obs"] * mesh.shape["chan"]
+    plan = shared_columns if BLOCK % device_count == 0 else exchange_per_step
     in_specs = (P("obs", "chan", None), P("chan", "obs"), P("chan", "obs"), P("obs"), P("obs"), P())
     out_specs = (P("obs", None), P("obs", None))
-    return jax.shard_map(
-        per_device, mesh=mesh, in_specs=in_specs, out_specs=out_specs, check_vma=False
-    )
+    return jax.shard_map(plan, mesh=mesh, in_specs=in_specs, out_specs=out_specs, check_vma=False)

time: 708 us -> 179 us (0.25)
  the two profiles are of different devices: /device:TPU:0 before, /device:TPU:15 now
where the time goes in v1:
time: 179 us; the launch traced here: 178 us
  Pallas kernels  57.7 us (32%)
  local copies, waits for them, and re-layouts  56.5 us (32%)
  blocking collectives  50.4 us (28%)
  starting transfers between devices  6.24 us (3%)
  other arithmetic  4.43 us (2%)
  between operations  2.03 us (1%)
    pallas_call x1, Pallas kernels, shared_columns(): pl.pallas_call(functools.partial(cg_kernel, obs_count, chan_count), out_s...  57.7 us
    unnamed x1, blocking collectives  50.4 us
    reshape x1, local copies, waits for them, and re-layouts, shared_columns(): packed.reshape(block_count, device_count, share * group_channels * padded)  8.95 us
    reshape x1, local copies, waits for them, and re-layouts, shared_columns(): packed.reshape(obs_count, halves, chan_count // halves, block_count * sha...  7.04 us
    unnamed x11, local copies, waits for them, and re-layouts  6.95 us
    transpose x1, local copies, waits for them, and re-layouts, shared_columns(): jac = packed.transpose(2, 4, 5, 1, 0, 3).reshape(-1, padded, halves * cols)  6.49 us
    reshape x1, local copies, waits for them, and re-layouts, shared_columns(): packed = packed.transpose(1, 0, 2).reshape(device_count, -1, 128)  6.47 us
    all_to_all x1, starting transfers between devices, shared_columns(): lax.all_to_all(packed, ('obs', 'chan'), split_axis=0, concat_axis=0, tile...  6.24 us
  transfers between devices with their start and end apart: 1, of which 0 were waited for; matrix products, arithmetic and copies ran while one was open for 3% of the time, Pallas kernels for 0%

profile of v1, /device:TPU:15, one launch (start us, length us, event | category | flops | bytes accessed | tf_op | source)
XLA Modules:
  0.0 177.7 jit_solution(6104433220206251926)
XLA Ops:
  1.3 0.8 fusion.2
  2.1 0.8 fusion.4
  2.8 2.0 %pad_maximum_fusion = bf16[256,32,140]{0,1,2:T(8,128)(2,1)S(1)} fusion(bf16[256,32,1]{0,1,2:T(8,128)(2,1)S(1)} %get-tuple-element.7, bf16[256,32,1]{0,1,2:T(8,128)(2,1)S(1)} %get-tuple-element.6, bf16[256,32,1]{0,1,2:T(8,128)(2,1)S(1)} %fusion.2, bf16[256,32,137]{0,1,2:T(8,128)(2,1)} %param.6), kind=kLoop, calls=%fused_computation | loop fusion | flops 3440640 | bytes 4587520 | tf_op jit(solution)/shard_map/concatenate | solution.py:268
  4.9 6.0 %copy.20 = bf16[256,32,140]{2,1,0:T(8,128)(2,1)} copy(bf16[256,32,140]{0,1,2:T(8,128)(2,1)S(1)} %pad_maximum_fusion) | data formatting | bytes 4587520
  10.9 5.3 %pad.11.clone = bf16[256,32,144]{2,1,0:T(8,128)(2,1)} pad(bf16[256,32,140]{2,1,0:T(8,128)(2,1)} %copy.20, bf16[]{:T(256)} %constant.3.clone.1), padding=0_0x0_0x0_4 | pad | bytes 4653058 | tf_op jit(solution)/shard_map/jit(_pad)/pad | solution.py:269
  16.2 8.9 %reshape.54 = bf16[2,32,18432]{2,1,0:T(8,128)(2,1)S(1)} reshape(bf16[256,32,144]{2,1,0:T(8,128)(2,1)} %pad.11.clone) | data formatting | bytes 4718592 | tf_op jit(solution)/shard_map/reshape | solution.py:270
  25.1 3.8 %copy.13 = bf16[32,2,18432]{2,1,0:T(2,128)(2,1)} copy(bf16[32,2,18432]{2,0,1:T(8,128)(2,1)S(1)} %bitcast.41) | data formatting | bytes 4718592 | tf_op jit(solution)/shard_map/transpose | solution.py:271
  29.0 6.5 %reshape.55 = bf16[32,288,128]{2,1,0:T(8,128)(2,1)} reshape(bf16[32,2,18432]{2,1,0:T(2,128)(2,1)} %copy.13) | data formatting | bytes 4718592 | tf_op jit(solution)/shard_map/reshape | solution.py:271
  35.4 6.2 %all-to-all-start = ((bf16[32,288,128]{2,1,0:T(8,128)(2,1)}), bf16[32,288,128]{2,1,0:T(8,128)(2,1)S(1)}, u32[]{:S(2)}, u32[]{:S(2)}) async-start(bf16[32,288,128]{2,1,0:T(8,128)(2,1)} %reshape.55), calls=%async_computation | async-start | bytes 4718592 | tf_op jit(solution)/shard_map/all_to_all | solution.py:272
  41.7 0.6 dynamic-slice
  43.0 0.2 dynamic-update-slice
  43.2 50.4 %all-reduce.3 = s32[16]{0:T(128)S(1)} all-reduce(s32[16]{0:T(128)S(1)} %dynamic-update-slice), channel_id=1, replica_groups=mesh['obs'=8,'chan'=4] {'obs'}, use_global_device_ids=true, to_apply=%add.3 | all-reduce | flops 16 | bytes 128
  93.8 0.3 convert_element_type.34
  94.1 0.6 add_convert_fusion
  94.7 0.7 copy.17.pick_ref
  95.5 0.5 fusion.6
  96.0 0.7 pad.12.gram_ref
  96.7 0.7 pad.13.cov_ref
  97.4 7.0 %reshape.56 = bf16[8,2,2,8,32,144]{5,4,3,2,1,0:T(8,128)(2,1)} reshape(bf16[32,288,128]{2,1,0:T(8,128)(2,1)S(1)} %all-to-all-done) | data formatting | bytes 4718592 | tf_op jit(solution)/shard_map/reshape | solution.py:273
  104.4 6.5 %copy.14 = bf16[2,32,144,2,8,8]{2,5,4,3,1,0:T(8,128)(2,1)} copy(bf16[2,32,144,2,8,8]{2,1,5,0,3,4:T(8,128)(2,1)} %bitcast.39) | data formatting | bytes 4718592 | tf_op jit(solution)/shard_map/transpose | solution.py:276
  110.9 5.7 %copy.16.jac_ref = bf16[64,144,128]{2,1,0:T(8,128)(2,1)} copy(bf16[64,144,128]{1,2,0:T(8,128)(2,1)} %bitcast.40) | data formatting | bytes 4718592 | tf_op jit(solution)/shard_map/reshape | solution.py:276
  116.6 57.7 %shard_map.77 = (f32[256,137]{1,0:T(8,128)}, f32[256,137]{1,0:T(8,128)}) custom-call(bf16[64,144,128]{2,1,0:T(8,128)(2,1)} %copy.16.jac_ref, f32[144,144]{1,0:T(8,128)} %pad.12.gram_ref, f32[144,144]{1,0:T(8,128)} %pad.13.cov_ref, f32[64,128]{1,0:T(8,128)} %copy.17.pick_ref, f32[128,64]{1,0:T(8,128)} %get-tuple-element.8.take_ref), custom_call_target="tpu_custom_call" | custom-call | tf_op jit(solution)/shard_map/pallas_call | solution.py:291
  174.3 1.7 copy.18
  176.0 1.7 copy.19
  (13 shorter events, 0.3 us)
Async XLA Ops:
  35.4 6.3 %copy-start.2 = (u32[32]{0:T(128)S(1)}, u32[32]{0:T(128)}, u32[]{:S(2)}) copy-start(u32[32]{0:T(128)} %constant.15) | copy-start | bytes 388
  35.4 7.5 %copy-start.1 = (s32[2]{0:T(128)S(1)}, s32[2]{0:T(128)}, u32[]{:S(2)}) copy-start(s32[2]{0:T(128)} %param.10) | copy-start | bytes 28
  35.4 60.0 %copy-start = (f32[137,137]{1,0:T(8,128)S(1)}, f32[137,137]{1,0:T(8,128)}, u32[]{:S(2)}) copy-start(f32[137,137]{1,0:T(8,128)} %param.11) | copy-start | bytes 225232
  35.4 61.9 %all-to-all-start = ((bf16[32,288,128]{2,1,0:T(8,128)(2,1)}), bf16[32,288,128]{2,1,0:T(8,128)(2,1)S(1)}, u32[]{:S(2)}, u32[]{:S(2)}) async-start(bf16[32,288,128]{2,1,0:T(8,128)(2,1)} %reshape.55), calls=%async_computation | async-start | bytes 4718592 | tf_op jit(solution)/shard_map/all_to_all | solution.py:272

commit v2 on v1

--- a/solution.py
+++ b/solution.py
@@ -120,16 +120,23 @@
     return (increment.reshape(-1, layers), residual.reshape(-1, layers))
 
 
+LANES = 128
+REST = 16
+
+
 def cg_kernel(
-    obs_count, chan_count, jac_ref, gram_ref, cov_ref, pick_ref, take_ref, increment_ref,
-    residual_ref, weight_ref, parts_ref, back_ref, sum_send, sum_recv, back_send, back_recv
+    obs_count, chan_count, jac_ref, rest_ref, gram_ref, cov_ref, increment_ref, residual_ref,
+    got_ref, got_rest_ref, wide_ref, turned_ref, weight_ref, parts_ref, back_ref,
+    jac_send, jac_recv, rest_send, rest_recv, own_sem, sum_send, sum_recv, back_send, back_recv
 ):
     device_count = obs_count * chan_count
     me = lax.axis_index("obs") * chan_count + lax.axis_index("chan")
-    rows, padded, lanes = jac_ref.shape
     layers = increment_ref.shape[1]
-    share = BLOCK // device_count
-    grid_cols = take_ref.shape[1]
+    block_count, share, channels = got_ref.shape[1:4]
+    mine = block_count * share
+    rows, padded, _ = turned_ref.shape
+    lows = chan_count // 2
+    grid_cols = GRID_BLK * obs_count * share
     piece = GRID_BLK * share
 
     def coords(target):
@@ -145,30 +152,123 @@
 
     lax.fori_loop(1, device_count, greet, 0)
 
+    def own_part(block, target):
+        return jac_ref.at[pl.ds(block * BLOCK + target * share, share), :, pl.ds(0, LANES)]
+
+    own = [
+        pltpu.make_async_copy(own_part(k, me), got_ref.at[me, k], own_sem.at[k])
+        for k in range(block_count)
+    ]
+    own.append(pltpu.make_async_copy(rest_ref.at[me], got_rest_ref.at[me], own_sem.at[block_count]))
+    for copy in own:
+        copy.start()
+    pl.semaphore_wait(barrier, device_count - 1)
+
+    def send_columns(offset, carry):
+        target = (me + offset) % device_count
+        for k in range(block_count):
+            pltpu.make_async_remote_copy(
+                src_ref=own_part(k, target),
+                dst_ref=got_ref.at[me, k],
+                send_sem=jac_send,
+                recv_sem=jac_recv,
+                device_id=coords(target),
+                device_id_type=MESH,
+            ).start()
+        pltpu.make_async_remote_copy(
+            src_ref=rest_ref.at[target],
+            dst_ref=got_rest_ref.at[me],
+            send_sem=rest_send,
+            recv_sem=rest_recv,
+            device_id=coords(target),
+            device_id_type=MESH,
+        ).start()
+        return carry
+
+    lax.fori_loop(1, device_count, send_columns, 0)
+    for copy in own:
+        copy.wait()
+
+    def wait_others(ref, sem):
+        others = ref.at[pl.ds(0, device_count - 1)]
+        pltpu.make_async_copy(others, others, sem).wait()
+
+    wait_others(got_rest_ref, rest_recv)
+    wait_others(got_rest_ref, rest_send)
+    wait_others(got_ref, jac_recv)
+    wait_others(got_ref, jac_send)
+
+    def widen(source, carry):
+        part = got_ref[source].astype(jnp.float32)
+        wide_ref[pl.ds(source * mine * channels, mine * channels), :] = part.reshape(-1, LANES)
+        return carry
+
+    lax.fori_loop(0, device_count, widen, 0)
+
+    def source_of(half, obs, low):
+        return obs * chan_count + half * lows + low
+
+    for low in range(lows):
+
+        def turn(n, carry, low=low):
+            picked = [
+                wide_ref[pl.ds(source_of(half, obs, low) * mine * channels + n, mine, stride=channels), :]
+                for half in range(2)
+                for obs in range(obs_count)
+            ]
+            turned_ref[low * channels + n, 0:LANES, :] = jnp.concatenate(picked, axis=0).T
+            return carry
+
+        lax.fori_loop(0, channels, turn, 0, unroll=2)
+        for half_rows in range(2):
+            picked = [
+                got_rest_ref[source_of(half, obs, low)].astype(jnp.float32)[
+                    half_rows * mine : (half_rows + 1) * mine
+                ]
+                for half in range(2)
+                for obs in range(obs_count)
+            ]
+            flipped = jnp.concatenate(picked, axis=0).T
+            for n in range(channels // 2):
+                turned_ref[low * channels + half_rows * (channels // 2) + n, LANES:padded, :] = (
+                    flipped[n * REST : (n + 1) * REST]
+                )
+
     def dot(a, b):
         return jnp.dot(a, b, precision=HIGHEST, preferred_element_type=jnp.float32)
 
+    ids = turned_ref[0, layers + 3 : layers + 4, :].astype(jnp.int32)
+    lane = lax.broadcasted_iota(jnp.int32, (grid_cols, LANES), 1)
+    spot = lax.broadcasted_iota(jnp.int32, (grid_cols, LANES), 0)
+    pick = (spot == ids * share + lane % share).astype(jnp.float32)
+
+    def collect(terms):
+        return lax.dot_general(
+            terms, pick, (((1,), (1,)), ((), ())), precision=HIGHEST,
+            preferred_element_type=jnp.float32,
+        )
+
     def source_step(n, acc):
-        kernel = jac_ref[n].astype(jnp.float32)
+        kernel = turned_ref[n]
         weight_ref[pl.ds(n, 1), :] = kernel[layers : layers + 1] + kernel[layers + 1 : layers + 2]
         return acc + kernel * kernel[layers + 2 : layers + 3]
 
-    zero = jnp.zeros((padded, lanes), jnp.float32)
-    residual = dot(lax.fori_loop(0, rows, source_step, zero, unroll=4), take_ref[...])
+    zero = jnp.zeros((padded, LANES), jnp.float32)
+    residual = collect(lax.fori_loop(0, rows, source_step, zero, unroll=4))
 
     control = direction = image = None
     norm_last = step_last = None
     for step in range(ITERS):
         spread = dot(gram_ref[...], residual)
-        field = dot(spread, pick_ref[...])
+        field = dot(spread, pick)
 
         def normal_step(n, acc):
-            kernel = jac_ref[n].astype(jnp.float32)
+            kernel = turned_ref[n]
             predicted = jnp.sum(kernel * field, axis=0, keepdims=True)
             return acc + kernel * (predicted * weight_ref[pl.ds(n, 1), :])
 
         terms = lax.fori_loop(0, rows, normal_step, zero, unroll=4)
-        applied = residual + dot(terms, take_ref[...])
+        applied = residual + collect(terms)
         norm_part = jnp.sum(residual * spread, axis=0, keepdims=True)
         curve_part = jnp.sum(applied * spread, axis=0, keepdims=True)
         sub = lax.broadcasted_iota(jnp.int32, (8, grid_cols), 0)
@@ -176,8 +276,6 @@
         if grid_cols < 128:
             both = jnp.concatenate([both, jnp.zeros((8, 128 - grid_cols), jnp.float32)], axis=1)
         parts_ref[step, me] = both
-        if step == 0:
-            pl.semaphore_wait(barrier, device_count - 1)
 
         def send_sum(offset, carry, step=step):
             pltpu.make_async_remote_copy(
@@ -209,12 +307,12 @@
         residual = residual - length * image
         norm_last, step_last = norm_now, length
 
-    def turned(a, b):
+    def flip_dot(a, b):
         return lax.dot_general(
             a, b, (((0,), (0,)), ((), ())), precision=HIGHEST, preferred_element_type=jnp.float32
         )
 
-    outs = (turned(control, gram_ref[...]), turned(residual, cov_ref[...]))
+    outs = (flip_dot(control, gram_ref[...]), flip_dot(residual, cov_ref[...]))
     out_stage, landed = back_ref.at[0], back_ref.at[1]
     for which, value in enumerate(outs):
         for owner in range(obs_count):
@@ -249,38 +347,25 @@
 def shared_columns(jacobian, departures, obs_weights, column_count, grid_block, sqrt_cov):
     obs_count, chan_count = lax.axis_size("obs"), lax.axis_size("chan")
     device_count = obs_count * chan_count
-    capacity, group_channels, layers = jacobian.shape
+    capacity, channels, layers = jacobian.shape
     block_count = capacity // BLOCK
     share = BLOCK // device_count
-    padded = -(-(layers + 3) // 16) * 16
-    cols = obs_count * block_count * share
-    halves = 1
-    while halves * 2 * cols <= 128 and chan_count % (halves * 2) == 0:
-        halves *= 2
-    grid_total = GRID_BLK * obs_count
+    padded = LANES + REST
+    rows = channels * chan_count // 2
 
     observed = (jnp.arange(capacity, dtype=jnp.int32) < column_count[0]).astype(jnp.float32)
     weight = observed[:, None] * obs_weights.T
     weight_high = weight.astype(jnp.bfloat16)
     weight_low = (weight - weight_high.astype(jnp.float32)).astype(jnp.bfloat16)
     source = (weight * departures.T).astype(jnp.bfloat16)
-    extra = jnp.stack([weight_high, weight_low, source], axis=2)
-    packed = jnp.concatenate([jacobian, extra], axis=2)
-    packed = jnp.pad(packed, ((0, 0), (0, 0), (0, padded - layers - 3)))
-    packed = packed.reshape(block_count, device_count, share * group_channels * padded)
-    packed = packed.transpose(1, 0, 2).reshape(device_count, -1, 128)
-    packed = lax.all_to_all(packed, ("obs", "chan"), split_axis=0, concat_axis=0, tiled=True)
-    packed = packed.reshape(
-        obs_count, halves, chan_count // halves, block_count * share, group_channels, padded
+    ids = jnp.broadcast_to(jnp.repeat(grid_block, BLOCK)[:, None], weight.shape)
+    extra = jnp.stack([weight_high, weight_low, source, ids.astype(jnp.bfloat16)], axis=2)
+    rest = jnp.concatenate([jacobian[:, :, LANES:], extra], axis=2)
+    rest = jnp.pad(rest, ((0, 0), (0, 0), (0, padded - layers - 4)))
+    rest = rest.reshape(block_count, device_count, share, 2, channels // 2 * REST)
+    rest = rest.transpose(1, 3, 0, 2, 4).reshape(
+        device_count, 2 * block_count * share, channels // 2 * REST
     )
-    jac = packed.transpose(2, 4, 5, 1, 0, 3).reshape(-1, padded, halves * cols)
-
-    every_id = lax.all_gather(grid_block, "obs", axis=0, tiled=True)
-    hit = every_id[:, None] == jnp.arange(grid_total, dtype=jnp.int32)[None, :]
-    same = jnp.eye(share, dtype=jnp.bool_)
-    take = (hit[:, None, :, None] & same[None, :, None, :]).astype(jnp.float32)
-    take = take.reshape(cols, grid_total * share)
-    take = jnp.concatenate([take] * halves, axis=0)
     fill = padded - layers
     gram = jnp.dot(sqrt_cov.T, sqrt_cov, precision=HIGHEST)
     gram = jnp.pad(gram, ((0, fill), (0, fill)))
@@ -288,27 +373,49 @@
 
     out = jax.ShapeDtypeStruct((GRID_BLK * BLOCK, layers), jnp.float32)
     vmem = pl.BlockSpec(memory_space=pltpu.VMEM)
+    dma = pltpu.SemaphoreType.DMA
     return pl.pallas_call(
         functools.partial(cg_kernel, obs_count, chan_count),
         out_shape=(out, out),
-        in_specs=[vmem] * 5,
+        in_specs=[pl.BlockSpec(memory_space=pl.ANY)] + [vmem] * 3,
         out_specs=(vmem, vmem),
         scratch_shapes=[
-            pltpu.VMEM((jac.shape[0], jac.shape[2]), jnp.float32),
+            pltpu.VMEM((device_count, block_count, share, channels, LANES), jnp.bfloat16),
+            pltpu.VMEM(rest.shape, jnp.bfloat16),
+            pltpu.VMEM((device_count * block_count * share * channels, LANES), jnp.float32),
+            pltpu.VMEM((rows, padded, LANES), jnp.float32),
+            pltpu.VMEM((rows, LANES), jnp.float32),
             pltpu.VMEM((ITERS, device_count, 8, 128), jnp.float32),
             pltpu.VMEM((2, device_count, 2, GRID_BLK * share, layers), jnp.float32),
-            pltpu.SemaphoreType.DMA((ITERS,)),
-            pltpu.SemaphoreType.DMA((ITERS,)),
-            pltpu.SemaphoreType.DMA,
-            pltpu.SemaphoreType.DMA,
+            dma, dma, dma, dma,
+            dma((block_count + 1,)),
+            dma((ITERS,)),
+            dma((ITERS,)),
+            dma, dma,
         ],
-        compiler_params=pltpu.CompilerParams(collective_id=0, has_side_effects=True),
-    )(jac, gram, cov, take.T, take)
+        compiler_params=pltpu.CompilerParams(
+            collective_id=0, has_side_effects=True, vmem_limit_bytes=50 * 1024 * 1024
+        ),
+    )(jacobian, rest, gram, cov)
 
 
 def solution(mesh):
     device_count = mesh.shape["obs"] * mesh.shape["chan"]
-    plan = shared_columns if BLOCK % device_count == 0 else exchange_per_step
+
+    def plan(jacobian, departures, obs_weights, column_count, grid_block, sqrt_cov):
+        capacity, channels, layers = jacobian.shape
+        mine = capacity // device_count
+        fits = (
+            BLOCK % device_count == 0
+            and mine == 8
+            and 2 * mesh.shape["obs"] * mine == LANES
+            and mesh.shape["chan"] % 2 == 0
+            and channels % 16 == 0
+            and LANES < layers <= LANES + REST - 4
+        )
+        chosen = shared_columns if fits else exchange_per_step
+        return chosen(jacobian, departures, obs_weights, column_count, grid_block, sqrt_cov)
+
     in_specs = (P("obs", "chan", None), P("chan", "obs"), P("chan", "obs"), P("obs"), P("obs"), P())
     out_specs = (P("obs", None), P("obs", None))
     return jax.shard_map(plan, mesh=mesh, in_specs=in_specs, out_specs=out_specs, check_vma=False)

time: 179 us -> 143 us (0.80)
  Pallas kernels: 57.7 us -> 118 us
  blocking collectives: 50.4 us -> 0 us
  local copies, waits for them, and re-layouts: 56.5 us -> 18.6 us
  starting transfers between devices: 6.24 us -> 0 us
    pallas_call x1, Pallas kernels: 57.7 us -> 118 us  [shared_columns(): pl.pallas_call(functools.partial(cg_kernel, obs_count, chan_count), out_s...]
    unnamed x1 -> x0, blocking collectives: 50.4 us -> none
    reshape x4 -> x2, local copies, waits for them, and re-layouts: 28.2 us -> 3.81 us  [the longest x1 3.74 us: shared_columns(): rest.reshape(block_count, device_count, share, 2, channels // 2 * REST)]
    transpose x3 -> x1, local copies, waits for them, and re-layouts: 11 us -> 0.1 us  [shared_columns(): rest.transpose(1, 3, 0, 2, 4)]
    all_to_all x1 -> x0, starting transfers between devices: 6.24 us -> none  [shared_columns(): lax.all_to_all(packed, ('obs', 'chan'), split_axis=0, concat_axis=0, tile...]
    unnamed x11 -> x6, local copies, waits for them, and re-layouts: 6.95 us -> 11.3 us
    pad x1, local copies, waits for them, and re-layouts: 5.29 us -> 1.75 us  [shared_columns(): rest = jnp.pad(rest, ((0, 0), (0, 0), (0, padded - layers - 4)))]
    concatenate x2 -> x0, other arithmetic: 2.66 us -> none  [the longest x1 2.03 us: shared_columns(): packed = jnp.concatenate([jacobian, extra], axis=2)]
  transfers between devices with their start and end apart: 1 -> 0, of which waited for: 0 -> 0; matrix products, arithmetic and copies ran while one was open for 3% -> 0% of each run, Pallas kernels for 0% -> 0%
where the time goes in v2:
time: 143 us
  Pallas kernels  118 us (83%)
  local copies, waits for them, and re-layouts  18.6 us (13%)
  other arithmetic  2.98 us (2%)
  matrix products  1.48 us (1%)
    pallas_call x1, Pallas kernels, shared_columns(): pl.pallas_call(functools.partial(cg_kernel, obs_count, chan_count), out_s...  118 us
    unnamed x6, local copies, waits for them, and re-layouts  11.3 us
    reshape x1, local copies, waits for them, and re-layouts, shared_columns(): rest.reshape(block_count, device_count, share, 2, channels // 2 * REST)  3.74 us

profile of v2, /device:TPU:15, one launch (start us, length us, event | category | flops | bytes accessed | tf_op | source)
XLA Modules:
  0.0 142.8 jit_solution(11442040670275443739)
XLA Ops:
  1.3 0.7 convert_element_type.37
  1.9 0.1 broadcast_bitcast_fusion
  2.0 1.0 copy.14
  3.1 1.5 %fusion.8 = f32[137,137]{1,0:T(8,128)S(1)} fusion(f32[137,137]{1,0:T(8,128)} %param.11), kind=kOutput, calls=%fused_computation.15 | convolution fusion | flops 30856236 | bytes 150152 | tf_op jit(solution)/shard_map/dot_general | solution.py:370
  4.6 0.9 slice_dynamic-update-slice_fusion
  5.5 0.8 fusion.3
  6.3 0.8 fusion.5
  7.0 0.8 fusion.7
  7.8 3.4 %copy.18 = bf16[256,32,13]{2,1,0:T(8,128)(2,1)S(1)} copy(bf16[256,32,13]{0,1,2:T(8,128)(2,1)S(1)} %constant_dynamic-update-slice_fusion) | data formatting | bytes 425984
  11.2 1.8 %pad.11.clone = bf16[256,32,16]{2,1,0:T(8,128)(2,1)} pad(bf16[256,32,13]{2,1,0:T(8,128)(2,1)S(1)} %copy.18, bf16[]{:T(256)} %constant.3.clone.1), padding=0_0x0_0x0_3 | pad | bytes 475138 | tf_op jit(solution)/shard_map/jit(_pad)/pad | solution.py:364
  13.0 0.0 copy-start
  13.0 3.7 %reshape.17 = bf16[2,32,4,2,256]{4,3,2,1,0:T(2,128)(2,1)S(1)} reshape(bf16[256,32,16]{2,1,0:T(8,128)(2,1)} %pad.11.clone) | data formatting | bytes 524288 | tf_op jit(solution)/shard_map/reshape | solution.py:365
  16.7 0.1 copy.13
  16.8 0.1 reshape.18.rest_ref
  16.9 0.0 copy-done
  16.9 6.0 %copy.15.jac_ref = bf16[256,32,137]{2,1,0:T(8,128)(2,1)} copy(bf16[256,32,137]{0,1,2:T(8,128)(2,1)S(1)} %copy-done) | data formatting | bytes 4489216 | tf_op args[0]
  22.9 118.4 %shard_map.77 = (f32[256,137]{1,0:T(8,128)S(1)}, f32[256,137]{1,0:T(8,128)S(1)}) custom-call(bf16[256,32,137]{2,1,0:T(8,128)(2,1)} %copy.15.jac_ref, bf16[32,16,256]{2,1,0:T(8,128)(2,1)S(1)} %reshape.18.rest_ref, f32[144,144]{1,0:T(8,128)S(1)} %pad.12.gram_ref, f32[144,144]{1,0:T(8,128)S(1)} %pad.13.cov_ref), custom_call_target="tpu_custom_call" | custom-call | tf_op jit(solution)/shard_map/pallas_call | solution.py:377
  141.3 0.8 copy.16
  142.0 0.8 copy.17
  (4 shorter events, 0.0 us)
Async XLA Ops:
  13.0 3.9 %copy-start = (bf16[256,32,137]{0,1,2:T(8,128)(2,1)S(1)}, bf16[256,32,137]{0,1,2:T(8,128)(2,1)}, u32[]{:S(2)}) copy-start(bf16[256,32,137]{0,1,2:T(8,128)(2,1)} %param.6) | copy-start | bytes 6733828

commit v3 on v2

--- a/solution.py
+++ b/solution.py
@@ -126,13 +126,14 @@
 
 def cg_kernel(
     obs_count, chan_count, jac_ref, rest_ref, gram_ref, cov_ref, increment_ref, residual_ref,
-    got_ref, got_rest_ref, wide_ref, turned_ref, weight_ref, parts_ref, back_ref,
+    got_ref, put_rest_ref, got_rest_ref, wide_ref, turned_ref, weight_ref, parts_ref, back_ref,
     jac_send, jac_recv, rest_send, rest_recv, own_sem, sum_send, sum_recv, back_send, back_recv
 ):
     device_count = obs_count * chan_count
     me = lax.axis_index("obs") * chan_count + lax.axis_index("chan")
     layers = increment_ref.shape[1]
-    block_count, share, channels = got_ref.shape[1:4]
+    _, _, block_count, share, half_channels, _ = got_ref.shape
+    channels = 2 * half_channels
     mine = block_count * share
     rows, padded, _ = turned_ref.shape
     lows = chan_count // 2
@@ -152,31 +153,42 @@
 
     lax.fori_loop(1, device_count, greet, 0)
 
-    def own_part(block, target):
-        return jac_ref.at[pl.ds(block * BLOCK + target * share, share), :, pl.ds(0, LANES)]
+    def own_part(part, block, target):
+        return jac_ref.at[
+            pl.ds(block * BLOCK + target * share, share), pl.ds(part * half_channels, half_channels), :
+        ]
 
     own = [
-        pltpu.make_async_copy(own_part(k, me), got_ref.at[me, k], own_sem.at[k])
+        pltpu.make_async_copy(
+            own_part(part, k, me), got_ref.at[part, me, k], own_sem.at[part * block_count + k]
+        )
+        for part in range(2)
         for k in range(block_count)
     ]
-    own.append(pltpu.make_async_copy(rest_ref.at[me], got_rest_ref.at[me], own_sem.at[block_count]))
     for copy in own:
         copy.start()
     pl.semaphore_wait(barrier, device_count - 1)
 
-    def send_columns(offset, carry):
+    def send_columns(part):
+        def send(offset, carry):
+            target = (me + offset) % device_count
+            for k in range(block_count):
+                pltpu.make_async_remote_copy(
+                    src_ref=own_part(part, k, target),
+                    dst_ref=got_ref.at[part, me, k],
+                    send_sem=jac_send.at[part],
+                    recv_sem=jac_recv.at[part],
+                    device_id=coords(target),
+                    device_id_type=MESH,
+                ).start()
+            return carry
+
+        lax.fori_loop(1, device_count, send, 0)
+
+    def send_rest(offset, carry):
         target = (me + offset) % device_count
-        for k in range(block_count):
-            pltpu.make_async_remote_copy(
-                src_ref=own_part(k, target),
-                dst_ref=got_ref.at[me, k],
-                send_sem=jac_send,
-                recv_sem=jac_recv,
-                device_id=coords(target),
-                device_id_type=MESH,
-            ).start()
         pltpu.make_async_remote_copy(
-            src_ref=rest_ref.at[target],
+            src_ref=put_rest_ref.at[target],
             dst_ref=got_rest_ref.at[me],
             send_sem=rest_send,
             recv_sem=rest_recv,
@@ -185,7 +197,22 @@
         ).start()
         return carry
 
-    lax.fori_loop(1, device_count, send_columns, 0)
+    send_columns(0)
+    columns = block_count * BLOCK
+    row = lax.broadcasted_iota(jnp.int32, (columns, columns), 0)
+    column = lax.broadcasted_iota(jnp.int32, (columns, columns), 1)
+    wanted = (row % mine) // share * BLOCK + row // mine * share + row % share
+    order = jnp.where(column == wanted, 1.0, 0.0).astype(jnp.bfloat16)
+    ordered = lax.dot_general(
+        order, rest_ref[...], (((1,), (1,)), ((), ())), preferred_element_type=jnp.float32
+    )
+    width = half_channels * REST
+    for part in range(2):
+        strip = ordered[:, part * width : (part + 1) * width].astype(jnp.bfloat16)
+        put_rest_ref[:, part * mine : (part + 1) * mine, :] = strip.reshape(device_count, mine, width)
+    got_rest_ref[me] = put_rest_ref[me]
+    lax.fori_loop(1, device_count, send_rest, 0)
+    send_columns(1)
     for copy in own:
         copy.wait()
 
@@ -195,44 +222,49 @@
 
     wait_others(got_rest_ref, rest_recv)
     wait_others(got_rest_ref, rest_send)
-    wait_others(got_ref, jac_recv)
-    wait_others(got_ref, jac_send)
-
-    def widen(source, carry):
-        part = got_ref[source].astype(jnp.float32)
-        wide_ref[pl.ds(source * mine * channels, mine * channels), :] = part.reshape(-1, LANES)
-        return carry
-
-    lax.fori_loop(0, device_count, widen, 0)
+
+    def widen(part):
+        def step(source, carry):
+            block = got_ref[part, source].astype(jnp.float32).reshape(-1, LANES)
+            wide_ref[pl.ds(source * mine * half_channels, mine * half_channels), :] = block
+            return carry
+
+        lax.fori_loop(0, device_count, step, 0)
 
     def source_of(half, obs, low):
         return obs * chan_count + half * lows + low
 
-    for low in range(lows):
-
-        def turn(n, carry, low=low):
+    def turn_half(part, low):
+        first = low * channels + part * half_channels
+
+        def turn(n, carry):
             picked = [
-                wide_ref[pl.ds(source_of(half, obs, low) * mine * channels + n, mine, stride=channels), :]
-                for half in range(2)
-                for obs in range(obs_count)
-            ]
-            turned_ref[low * channels + n, 0:LANES, :] = jnp.concatenate(picked, axis=0).T
-            return carry
-
-        lax.fori_loop(0, channels, turn, 0, unroll=2)
-        for half_rows in range(2):
-            picked = [
-                got_rest_ref[source_of(half, obs, low)].astype(jnp.float32)[
-                    half_rows * mine : (half_rows + 1) * mine
+                wide_ref[
+                    pl.ds(source_of(half, obs, low) * mine * half_channels + n, mine, stride=half_channels), :
                 ]
                 for half in range(2)
                 for obs in range(obs_count)
             ]
-            flipped = jnp.concatenate(picked, axis=0).T
-            for n in range(channels // 2):
-                turned_ref[low * channels + half_rows * (channels // 2) + n, LANES:padded, :] = (
-                    flipped[n * REST : (n + 1) * REST]
-                )
+            turned_ref[first + n, 0:LANES, :] = jnp.concatenate(picked, axis=0).T
+            return carry
+
+        lax.fori_loop(0, half_channels, turn, 0, unroll=2)
+        picked = [
+            got_rest_ref[source_of(half, obs, low)].astype(jnp.float32)[part * mine : (part + 1) * mine]
+            for half in range(2)
+            for obs in range(obs_count)
+        ]
+        flipped = jnp.concatenate(picked, axis=0).T
+        for n in range(half_channels):
+            turned_ref[first + n, LANES:padded, :] = flipped[n * REST : (n + 1) * REST]
+
+    for part in range(2):
+        others = got_ref.at[part, pl.ds(0, device_count - 1)]
+        pltpu.make_async_copy(others, others, jac_recv.at[part]).wait()
+        pltpu.make_async_copy(others, others, jac_send.at[part]).wait()
+        widen(part)
+        for low in range(lows):
+            turn_half(part, low)
 
     def dot(a, b):
         return jnp.dot(a, b, precision=HIGHEST, preferred_element_type=jnp.float32)
@@ -242,11 +274,26 @@
     spot = lax.broadcasted_iota(jnp.int32, (grid_cols, LANES), 0)
     pick = (spot == ids * share + lane % share).astype(jnp.float32)
 
+    def times(a, b, b_dim):
+        total = None
+        for _ in range(3):
+            part = a.astype(jnp.bfloat16)
+            a = a - part.astype(jnp.float32)
+            product = lax.dot_general(
+                part, b, (((1,), (b_dim,)), ((), ())), preferred_element_type=jnp.float32
+            )
+            total = product if total is None else total + product
+        return total
+
+    picked_bf16 = pick.astype(jnp.bfloat16)
+    shared = lax.dot_general(
+        picked_bf16, picked_bf16, (((0,), (0,)), ((), ())), preferred_element_type=jnp.float32
+    )
+    copies = jnp.sum(shared, axis=0, keepdims=True)
+    shared = shared.astype(jnp.bfloat16)
+
     def collect(terms):
-        return lax.dot_general(
-            terms, pick, (((1,), (1,)), ((), ())), precision=HIGHEST,
-            preferred_element_type=jnp.float32,
-        )
+        return times(terms, shared, 0)
 
     def source_step(n, acc):
         kernel = turned_ref[n]
@@ -256,26 +303,24 @@
     zero = jnp.zeros((padded, LANES), jnp.float32)
     residual = collect(lax.fori_loop(0, rows, source_step, zero, unroll=4))
 
-    control = direction = image = None
+    def normal(field, spread):
+        def normal_step(n, acc):
+            kernel = turned_ref[n]
+            predicted = jnp.sum(kernel * spread, axis=0, keepdims=True)
+            return acc + kernel * (predicted * weight_ref[pl.ds(n, 1), :])
+
+        return field + collect(lax.fori_loop(0, rows, normal_step, zero, unroll=4))
+
+    share_of = 1.0 / copies
+    spread = dot(gram_ref[...], residual)
+    applied = normal(residual, spread)
+    control = direction = image = spread_image = image_applied = None
     norm_last = step_last = None
     for step in range(ITERS):
-        spread = dot(gram_ref[...], residual)
-        field = dot(spread, pick)
-
-        def normal_step(n, acc):
-            kernel = turned_ref[n]
-            predicted = jnp.sum(kernel * field, axis=0, keepdims=True)
-            return acc + kernel * (predicted * weight_ref[pl.ds(n, 1), :])
-
-        terms = lax.fori_loop(0, rows, normal_step, zero, unroll=4)
-        applied = residual + collect(terms)
-        norm_part = jnp.sum(residual * spread, axis=0, keepdims=True)
-        curve_part = jnp.sum(applied * spread, axis=0, keepdims=True)
-        sub = lax.broadcasted_iota(jnp.int32, (8, grid_cols), 0)
-        both = jnp.where(sub == 0, norm_part, jnp.where(sub == 1, curve_part, 0.0))
-        if grid_cols < 128:
-            both = jnp.concatenate([both, jnp.zeros((8, 128 - grid_cols), jnp.float32)], axis=1)
-        parts_ref[step, me] = both
+        norm_part = jnp.sum(residual * spread, axis=0, keepdims=True) * share_of
+        curve_part = jnp.sum(applied * spread, axis=0, keepdims=True) * share_of
+        sub = lax.broadcasted_iota(jnp.int32, (8, LANES), 0)
+        parts_ref[step, me] = jnp.where(sub == 0, norm_part, jnp.where(sub == 1, curve_part, 0.0))
 
         def send_sum(offset, carry, step=step):
             pltpu.make_async_remote_copy(
@@ -289,6 +334,10 @@
             return carry
 
         lax.fori_loop(1, device_count, send_sum, 0)
+        last = step == ITERS - 1
+        if not last:
+            next_spread = dot(gram_ref[...], applied)
+            next_applied = normal(applied, next_spread)
         others = parts_ref.at[step, pl.ds(0, device_count - 1)]
         pltpu.make_async_copy(others, others, sum_recv.at[step]).wait()
         pltpu.make_async_copy(others, others, sum_send.at[step]).wait()
@@ -297,15 +346,24 @@
         if step == 0:
             length = norm_now / curve
             direction, image = residual, applied
+            spread_image, image_applied = next_spread, next_applied
             control = length * direction
         else:
             ratio = norm_now / norm_last
             length = norm_now / (curve - ratio * norm_now / step_last)
             direction = residual + ratio * direction
             image = applied + ratio * image
+            if not last:
+                spread_image = next_spread + ratio * spread_image
+                image_applied = next_applied + ratio * image_applied
             control = control + length * direction
         residual = residual - length * image
+        if not last:
+            spread = spread - length * spread_image
+            applied = applied - length * image_applied
         norm_last, step_last = norm_now, length
+    control = times(control * share_of, picked_bf16, 1)
+    residual = times(residual * share_of, picked_bf16, 1)
 
     def flip_dot(a, b):
         return lax.dot_general(
@@ -354,18 +412,16 @@
     rows = channels * chan_count // 2
 
     observed = (jnp.arange(capacity, dtype=jnp.int32) < column_count[0]).astype(jnp.float32)
-    weight = observed[:, None] * obs_weights.T
+    weight = observed[None, :] * obs_weights
     weight_high = weight.astype(jnp.bfloat16)
     weight_low = (weight - weight_high.astype(jnp.float32)).astype(jnp.bfloat16)
-    source = (weight * departures.T).astype(jnp.bfloat16)
-    ids = jnp.broadcast_to(jnp.repeat(grid_block, BLOCK)[:, None], weight.shape)
-    extra = jnp.stack([weight_high, weight_low, source, ids.astype(jnp.bfloat16)], axis=2)
-    rest = jnp.concatenate([jacobian[:, :, LANES:], extra], axis=2)
-    rest = jnp.pad(rest, ((0, 0), (0, 0), (0, padded - layers - 4)))
-    rest = rest.reshape(block_count, device_count, share, 2, channels // 2 * REST)
-    rest = rest.transpose(1, 3, 0, 2, 4).reshape(
-        device_count, 2 * block_count * share, channels // 2 * REST
-    )
+    source = (weight * departures).astype(jnp.bfloat16)
+    ids = jnp.broadcast_to(jnp.repeat(grid_block, BLOCK)[None, :], weight.shape)
+    extra = jnp.stack([weight_high, weight_low, source, ids.astype(jnp.bfloat16)], axis=1)
+    rest = jnp.concatenate([jacobian[:, :, LANES:].transpose(1, 2, 0), extra], axis=1)
+    rest = jnp.pad(rest, ((0, 0), (0, padded - layers - 4), (0, 0)))
+    rest = rest.reshape(channels * REST, capacity)
+    rest_shape = (device_count, 2 * block_count * share, channels // 2 * REST)
     fill = padded - layers
     gram = jnp.dot(sqrt_cov.T, sqrt_cov, precision=HIGHEST)
     gram = jnp.pad(gram, ((0, fill), (0, fill)))
@@ -380,15 +436,16 @@
         in_specs=[pl.BlockSpec(memory_space=pl.ANY)] + [vmem] * 3,
         out_specs=(vmem, vmem),
         scratch_shapes=[
-            pltpu.VMEM((device_count, block_count, share, channels, LANES), jnp.bfloat16),
-            pltpu.VMEM(rest.shape, jnp.bfloat16),
-            pltpu.VMEM((device_count * block_count * share * channels, LANES), jnp.float32),
+            pltpu.VMEM((2, device_count, block_count, share, channels // 2, LANES), jnp.bfloat16),
+            pltpu.VMEM(rest_shape, jnp.bfloat16),
+            pltpu.VMEM(rest_shape, jnp.bfloat16),
+            pltpu.VMEM((device_count * block_count * share * channels // 2, LANES), jnp.float32),
             pltpu.VMEM((rows, padded, LANES), jnp.float32),
             pltpu.VMEM((rows, LANES), jnp.float32),
             pltpu.VMEM((ITERS, device_count, 8, 128), jnp.float32),
             pltpu.VMEM((2, device_count, 2, GRID_BLK * share, layers), jnp.float32),
-            dma, dma, dma, dma,
-            dma((block_count + 1,)),
+            dma((2,)), dma((2,)), dma, dma,
+            dma((2 * block_count,)),
             dma((ITERS,)),
             dma((ITERS,)),
             dma, dma,
@@ -396,7 +453,7 @@
         compiler_params=pltpu.CompilerParams(
             collective_id=0, has_side_effects=True, vmem_limit_bytes=50 * 1024 * 1024
         ),
-    )(jacobian, rest, gram, cov)
+    )(jacobian[:, :, :LANES], rest, gram, cov)
 
 
 def solution(mesh):
@@ -410,7 +467,7 @@
             and mine == 8
             and 2 * mesh.shape["obs"] * mine == LANES
             and mesh.shape["chan"] % 2 == 0
-            and channels % 16 == 0
+            and channels % 32 == 0
             and LANES < layers <= LANES + REST - 4
         )
         chosen = shared_columns if fits else exchange_per_step

time: 143 us -> 119 us (0.83)
  Pallas kernels: 118 us -> 106 us
  local copies, waits for them, and re-layouts: 18.6 us -> 10.3 us
  other arithmetic: 2.98 us -> 0.03 us
    pallas_call x1, Pallas kernels: 118 us -> 106 us  [shared_columns(): pl.pallas_call(functools.partial(cg_kernel, obs_count, chan_count), out_s...]
    unnamed x6 -> x12, local copies, waits for them, and re-layouts: 11.3 us -> 5.55 us
    reshape x2 -> x0, local copies, waits for them, and re-layouts: 3.81 us -> none  [the longest x1 3.74 us: shared_columns(): rest.reshape(block_count, device_count, share, 2, channels // 2 * REST)]
    slice x0 -> x1, local copies, waits for them, and re-layouts: none -> 3.09 us  [shared_columns(): jacobian[:, :, :LANES]]
    unnamed x3, other arithmetic: 2.31 us -> 0.02 us
    pad x1, local copies, waits for them, and re-layouts: 1.75 us -> 0.03 us  [shared_columns(): rest = jnp.pad(rest, ((0, 0), (0, padded - layers - 4), (0, 0)))]
where the time goes in v3:
time: 119 us; the launch traced here: 118 us
  Pallas kernels  106 us (89%)
  local copies, waits for them, and re-layouts  10.3 us (9%)
  between operations  1.42 us (1%)
    pallas_call x1, Pallas kernels, shared_columns(): pl.pallas_call(functools.partial(cg_kernel, obs_count, chan_count), out_s...  106 us
    unnamed x12, local copies, waits for them, and re-layouts  5.55 us
    slice x1, local copies, waits for them, and re-layouts, shared_columns(): jacobian[:, :, :LANES]  3.09 us

profile of v3, /device:TPU:15, one launch (start us, length us, event | category | flops | bytes accessed | tf_op | source)
XLA Modules:
  0.0 118.3 jit_solution(9177688056913225923)
XLA Ops:
  0.6 3.1 %slice.6 = bf16[256,32,128]{0,1,2:T(8,128)(2,1)} slice(bf16[256,32,137]{0,1,2:T(8,128)(2,1)} %param.6), slice={[0:256], [0:32], [0:128]} | slice | bytes 4194304 | tf_op jit(solution)/shard_map/slice | solution.py:456
  3.7 0.0 copy-start.1
  3.7 0.0 copy-start.2
  3.7 0.0 copy-start.3
  3.7 0.0 copy-start
  3.7 4.4 %copy.13.jac_ref = bf16[256,32,128]{2,1,0:T(8,128)(2,1)S(1)} copy(bf16[256,32,128]{0,1,2:T(8,128)(2,1)} %slice.6) | data formatting | bytes 4194304
  8.1 0.9 bitcast_dynamic-update-slice_fusion
  9.7 0.0 copy-done.1
  9.8 0.0 copy-done.2
  9.8 0.0 copy-done.3
  9.8 0.1 broadcast_bitcast_fusion
  9.9 0.1 copy.14
  10.0 0.0 copy-done
  10.1 0.5 fusion.6
  10.6 0.1 copy.10
  10.7 106.1 %shard_map.77 = (f32[256,137]{1,0:T(8,128)S(1)}, f32[256,137]{1,0:T(8,128)S(1)}) custom-call(bf16[256,32,128]{2,1,0:T(8,128)(2,1)S(1)} %copy.13.jac_ref, bf16[512,256]{1,0:T(8,128)(2,1)S(1)} %bitcast.22, f32[144,144]{1,0:T(8,128)S(1)} %pad.12.gram_ref, f32[144,144]{1,0:T(8,128)S(1)} %pad.13.cov_ref), custom_call_target="tpu_custom_call" | custom-call | tf_op jit(solution)/shard_map/pallas_call | solution.py:433
  116.8 0.8 copy.11
  117.6 0.8 copy.12
  (9 shorter events, 0.1 us)
Async XLA Ops:
  3.7 6.0 %copy-start.1 = (f32[32,256]{1,0:T(8,128)S(1)}, f32[32,256]{1,0:T(8,128)}, u32[]{:S(2)}) copy-start(f32[32,256]{1,0:T(8,128)} %param.8) | copy-start | bytes 98308
  3.7 6.0 %copy-start.2 = (f32[32,256]{1,0:T(8,128)S(1)}, f32[32,256]{1,0:T(8,128)}, u32[]{:S(2)}) copy-start(f32[32,256]{1,0:T(8,128)} %param.7) | copy-start | bytes 98308
  3.7 6.1 %copy-start.3 = (s32[2]{0:T(128)S(1)}, s32[2]{0:T(128)}, u32[]{:S(2)}) copy-start(s32[2]{0:T(128)} %param.10) | copy-start | bytes 28
  3.7 6.3 %copy-start = (f32[137,137]{1,0:T(8,128)S(1)}, f32[137,137]{1,0:T(8,128)}, u32[]{:S(2)}) copy-start(f32[137,137]{1,0:T(8,128)} %param.11) | copy-start | bytes 225232

commit v4 on v3

--- a/solution.py
+++ b/solution.py
@@ -122,6 +122,7 @@
 
 LANES = 128
 REST = 16
+STRIDE = 11
 
 
 def cg_kernel(
@@ -155,7 +156,7 @@
 
     def own_part(part, block, target):
         return jac_ref.at[
-            pl.ds(block * BLOCK + target * share, share), pl.ds(part * half_channels, half_channels), :
+            pl.ds(block * BLOCK + target * share, share), pl.ds(part * half_channels, half_channels), pl.ds(0, LANES)
         ]
 
     own = [
@@ -171,7 +172,7 @@
 
     def send_columns(part):
         def send(offset, carry):
-            target = (me + offset) % device_count
+            target = (me + offset * STRIDE) % device_count
             for k in range(block_count):
                 pltpu.make_async_remote_copy(
                     src_ref=own_part(part, k, target),
@@ -186,7 +187,7 @@
         lax.fori_loop(1, device_count, send, 0)
 
     def send_rest(offset, carry):
-        target = (me + offset) % device_count
+        target = (me + offset * STRIDE) % device_count
         pltpu.make_async_remote_copy(
             src_ref=put_rest_ref.at[target],
             dst_ref=got_rest_ref.at[me],
@@ -319,8 +320,10 @@
     for step in range(ITERS):
         norm_part = jnp.sum(residual * spread, axis=0, keepdims=True) * share_of
         curve_part = jnp.sum(applied * spread, axis=0, keepdims=True) * share_of
-        sub = lax.broadcasted_iota(jnp.int32, (8, LANES), 0)
-        parts_ref[step, me] = jnp.where(sub == 0, norm_part, jnp.where(sub == 1, curve_part, 0.0))
+        norm_part = jnp.sum(norm_part, axis=1, keepdims=True)
+        curve_part = jnp.sum(curve_part, axis=1, keepdims=True)
+        place = lax.broadcasted_iota(jnp.int32, (1, LANES), 1)
+        parts_ref[step, me] = jnp.where(place == 0, norm_part, jnp.where(place == 1, curve_part, 0.0))
 
         def send_sum(offset, carry, step=step):
             pltpu.make_async_remote_copy(
@@ -341,8 +344,9 @@
         others = parts_ref.at[step, pl.ds(0, device_count - 1)]
         pltpu.make_async_copy(others, others, sum_recv.at[step]).wait()
         pltpu.make_async_copy(others, others, sum_send.at[step]).wait()
-        total = jnp.sum(jnp.sum(parts_ref[step], axis=0), axis=1, keepdims=True)
-        norm_now, curve = total[0:1], total[1:2]
+        total = jnp.sum(parts_ref[step], axis=0)
+        norm_now = jnp.sum(jnp.where(place == 0, total, 0.0), axis=1, keepdims=True)
+        curve = jnp.sum(jnp.where(place == 1, total, 0.0), axis=1, keepdims=True)
         if step == 0:
             length = norm_now / curve
             direction, image = residual, applied
@@ -372,9 +376,9 @@
 
     outs = (flip_dot(control, gram_ref[...]), flip_dot(residual, cov_ref[...]))
     out_stage, landed = back_ref.at[0], back_ref.at[1]
-    for which, value in enumerate(outs):
-        for owner in range(obs_count):
-            out_stage[owner * chan_count, which, :, :] = value[owner * piece : (owner + 1) * piece, :layers]
+    for owner in range(obs_count):
+        pieces = [value[owner * piece : (owner + 1) * piece, :layers] for value in outs]
+        out_stage[owner * chan_count, :, :] = jnp.concatenate(pieces, axis=0).astype(jnp.bfloat16)
     landed[me] = out_stage[(me // chan_count) * chan_count]
 
     def send_back(offset, carry):
@@ -393,13 +397,13 @@
     others = landed.at[pl.ds(0, device_count - 1)]
     pltpu.make_async_copy(others, others, back_recv).wait()
     pltpu.make_async_copy(others, others, back_send).wait()
-    for which, out_ref in enumerate((increment_ref, residual_ref)):
-        for block in range(GRID_BLK):
-            for source in range(device_count):
+    for source in range(device_count):
+        block_rows = landed[source].astype(jnp.float32)
+        for which, out_ref in enumerate((increment_ref, residual_ref)):
+            for block in range(GRID_BLK):
                 first = block * BLOCK + source * share
-                out_ref[first : first + share, :] = landed[
-                    source, which, block * share : (block + 1) * share, :
-                ]
+                taken = which * piece + block * share
+                out_ref[first : first + share, :] = block_rows[taken : taken + share]
 
 
 def shared_columns(jacobian, departures, obs_weights, column_count, grid_block, sqrt_cov):
@@ -442,8 +446,8 @@
             pltpu.VMEM((device_count * block_count * share * channels // 2, LANES), jnp.float32),
             pltpu.VMEM((rows, padded, LANES), jnp.float32),
             pltpu.VMEM((rows, LANES), jnp.float32),
-            pltpu.VMEM((ITERS, device_count, 8, 128), jnp.float32),
-            pltpu.VMEM((2, device_count, 2, GRID_BLK * share, layers), jnp.float32),
+            pltpu.VMEM((ITERS, device_count, 1, LANES), jnp.float32),
+            pltpu.VMEM((2, device_count, 2 * GRID_BLK * share, layers), jnp.bfloat16),
             dma((2,)), dma((2,)), dma, dma,
             dma((2 * block_count,)),
             dma((ITERS,)),
@@ -453,7 +457,7 @@
         compiler_params=pltpu.CompilerParams(
             collective_id=0, has_side_effects=True, vmem_limit_bytes=50 * 1024 * 1024
         ),
-    )(jacobian[:, :, :LANES], rest, gram, cov)
+    )(jacobian, rest, gram, cov)
 
 
 def solution(mesh):

time: 119 us -> 111 us (0.933)
  Pallas kernels: 106 us -> 94.3 us
  other arithmetic: 0.03 us -> 2.98 us
    pallas_call x1, Pallas kernels: 106 us -> 94.3 us  [shared_columns(): pl.pallas_call(functools.partial(cg_kernel, obs_count, chan_count), out_s...]
    slice x1 -> x0, local copies, waits for them, and re-layouts: 3.09 us -> none  [shared_columns(): jacobian[:, :, :LANES]]
    unnamed x12 -> x6, local copies, waits for them, and re-layouts: 5.55 us -> 8.03 us
    unnamed x3, other arithmetic: 0.02 us -> 2.31 us
where the time goes in v4:
time: 111 us; the launch traced here: 110 us
  Pallas kernels  94.3 us (85%)
  local copies, waits for them, and re-layouts  9.69 us (9%)
  other arithmetic  2.98 us (3%)
  between operations  1.51 us (1%)
  matrix products  1.48 us (1%)
    pallas_call x1, Pallas kernels, shared_columns(): pl.pallas_call(functools.partial(cg_kernel, obs_count, chan_count), out_s...  94.3 us
    unnamed x6, local copies, waits for them, and re-layouts  8.03 us
    unnamed x3, other arithmetic  2.31 us

profile of v4, /device:TPU:15, one launch (start us, length us, event | category | flops | bytes accessed | tf_op | source)
XLA Modules:
  0.0 110.0 jit_solution(4344830409319533966)
XLA Ops:
  0.6 0.0 copy-start
  1.4 0.7 convert_element_type.37
  2.1 0.1 broadcast_bitcast_fusion
  2.2 1.0 copy.9
  3.2 1.5 %fusion.6 = f32[137,137]{1,0:T(8,128)S(1)} fusion(f32[137,137]{1,0:T(8,128)} %param.11), kind=kOutput, calls=%fused_computation.13 | convolution fusion | flops 30856236 | bytes 150152 | tf_op jit(solution)/shard_map/dot_general | solution.py:430
  4.7 0.9 bitcast_dynamic-update-slice_fusion
  5.7 0.8 fusion.1
  6.4 0.8 fusion.3
  7.2 0.8 fusion.5
  8.0 0.1 copy.13
  8.1 0.0 copy-done
  8.2 6.0 %copy.10.jac_ref = bf16[256,32,137]{2,1,0:T(8,128)(2,1)} copy(bf16[256,32,137]{0,1,2:T(8,128)(2,1)S(1)} %copy-done) | data formatting | bytes 4489216 | tf_op args[0]
  14.1 94.3 %shard_map.77 = (f32[256,137]{1,0:T(8,128)S(1)}, f32[256,137]{1,0:T(8,128)S(1)}) custom-call(bf16[256,32,137]{2,1,0:T(8,128)(2,1)} %copy.10.jac_ref, bf16[512,256]{1,0:T(8,128)(2,1)S(1)} %bitcast.22, f32[144,144]{1,0:T(8,128)S(1)} %pad.12.gram_ref, f32[144,144]{1,0:T(8,128)S(1)} %pad.13.cov_ref), custom_call_target="tpu_custom_call" | custom-call | tf_op jit(solution)/shard_map/pallas_call | solution.py:437
  108.4 0.8 copy.11
  109.2 0.8 copy.12
  (5 shorter events, 0.1 us)
Async XLA Ops:
  0.6 7.5 %copy-start = (bf16[256,32,137]{0,1,2:T(8,128)(2,1)S(1)}, bf16[256,32,137]{0,1,2:T(8,128)(2,1)}, u32[]{:S(2)}) copy-start(bf16[256,32,137]{0,1,2:T(8,128)(2,1)} %param.6) | copy-start | bytes 6733828

commit v5 on v4

--- a/solution.py
+++ b/solution.py
@@ -156,7 +156,7 @@
 
     def own_part(part, block, target):
         return jac_ref.at[
-            pl.ds(block * BLOCK + target * share, share), pl.ds(part * half_channels, half_channels), pl.ds(0, LANES)
+            pl.ds(block * BLOCK + target * share, share), pl.ds(part * half_channels, half_channels), :
         ]
 
     own = [
@@ -457,7 +457,7 @@
         compiler_params=pltpu.CompilerParams(
             collective_id=0, has_side_effects=True, vmem_limit_bytes=50 * 1024 * 1024
         ),
-    )(jacobian, rest, gram, cov)
+    )(jacobian[:, :, :LANES], rest, gram, cov)
 
 
 def solution(mesh):

time: 111 us -> 107 us (0.964)
  other arithmetic: 2.98 us -> 0.03 us
    slice x0 -> x1, local copies, waits for them, and re-layouts: none -> 3.09 us  [shared_columns(): jacobian[:, :, :LANES]]
    unnamed x6 -> x12, local copies, waits for them, and re-layouts: 8.03 us -> 5.55 us
    unnamed x3, other arithmetic: 2.31 us -> 0.02 us
where the time goes in v5:
time: 107 us
  Pallas kernels  94.4 us (88%)
  local copies, waits for them, and re-layouts  10.3 us (10%)
  between operations  1.42 us (1%)
    pallas_call x1, Pallas kernels, shared_columns(): pl.pallas_call(functools.partial(cg_kernel, obs_count, chan_count), out_s...  94.4 us
    unnamed x12, local copies, waits for them, and re-layouts  5.55 us
    slice x1, local copies, waits for them, and re-layouts, shared_columns(): jacobian[:, :, :LANES]  3.09 us

profile of v5, /device:TPU:15, one launch (start us, length us, event | category | flops | bytes accessed | tf_op | source)
XLA Modules:
  0.0 106.6 jit_solution(16363740943554548866)
XLA Ops:
  0.6 3.1 %slice.6 = bf16[256,32,128]{0,1,2:T(8,128)(2,1)} slice(bf16[256,32,137]{0,1,2:T(8,128)(2,1)} %param.6), slice={[0:256], [0:32], [0:128]} | slice | bytes 4194304 | tf_op jit(solution)/shard_map/slice | solution.py:460
  3.7 0.0 copy-start.1
  3.7 0.0 copy-start.2
  3.7 0.0 copy-start.3
  3.7 0.0 copy-start
  3.7 4.4 %copy.13.jac_ref = bf16[256,32,128]{2,1,0:T(8,128)(2,1)S(1)} copy(bf16[256,32,128]{0,1,2:T(8,128)(2,1)} %slice.6) | data formatting | bytes 4194304
  8.1 0.9 bitcast_dynamic-update-slice_fusion
  9.7 0.0 copy-done.1
  9.8 0.0 copy-done.2
  9.8 0.0 copy-done.3
  9.8 0.1 broadcast_bitcast_fusion
  9.9 0.1 copy.14
  10.0 0.0 copy-done
  10.1 0.5 fusion.6
  10.6 0.1 copy.10
  10.7 94.4 %shard_map.77 = (f32[256,137]{1,0:T(8,128)S(1)}, f32[256,137]{1,0:T(8,128)S(1)}) custom-call(bf16[256,32,128]{2,1,0:T(8,128)(2,1)S(1)} %copy.13.jac_ref, bf16[512,256]{1,0:T(8,128)(2,1)S(1)} %bitcast.22, f32[144,144]{1,0:T(8,128)S(1)} %pad.12.gram_ref, f32[144,144]{1,0:T(8,128)S(1)} %pad.13.cov_ref), custom_call_target="tpu_custom_call" | custom-call | tf_op jit(solution)/shard_map/pallas_call | solution.py:437
  105.1 0.8 copy.11
  105.8 0.8 copy.12
  (9 shorter events, 0.1 us)
Async XLA Ops:
  3.7 6.0 %copy-start.1 = (f32[32,256]{1,0:T(8,128)S(1)}, f32[32,256]{1,0:T(8,128)}, u32[]{:S(2)}) copy-start(f32[32,256]{1,0:T(8,128)} %param.8) | copy-start | bytes 98308
  3.7 6.0 %copy-start.2 = (f32[32,256]{1,0:T(8,128)S(1)}, f32[32,256]{1,0:T(8,128)}, u32[]{:S(2)}) copy-start(f32[32,256]{1,0:T(8,128)} %param.7) | copy-start | bytes 98308
  3.7 6.1 %copy-start.3 = (s32[2]{0:T(128)S(1)}, s32[2]{0:T(128)}, u32[]{:S(2)}) copy-start(s32[2]{0:T(128)} %param.10) | copy-start | bytes 28
  3.7 6.3 %copy-start = (f32[137,137]{1,0:T(8,128)S(1)}, f32[137,137]{1,0:T(8,128)}, u32[]{:S(2)}) copy-start(f32[137,137]{1,0:T(8,128)} %param.11) | copy-start | bytes 225232
